TPU v7x, 256 devices: a whole 4x4x8 slice. The times are simulated.
256 devices in a mesh: lon: 16 (over x_hi, y, core), dp: 16 (over z, x_lo).
Axes of the slice: x: 4 (x_hi: 2, x_lo: 2; x = x_hi * 2 + x_lo), y: 4, z: 8, core: 2. Of those that a mesh axis runs over, the one named last changes fastest.
Arguments:
- inputs: bfloat16 [16, 32, 768, 256], P('dp', None, 'lon'), may hold values from -6 to 6
- pre_act: bfloat16 [16, 32, 768, 256], P('dp', None, 'lon'), may hold values from -6 to 6
- cotangent: bfloat16 [16, 32, 768, 256], P('dp', None, 'lon'), may hold values from -6 to 6
- first_weight: bfloat16 [2304, 256], replicated, may hold values from -0.125 to 0.125
- second_weight: bfloat16 [2304, 256], replicated, may hold values from -0.125 to 0.125
Outputs:
- input_gradient_array: bfloat16 [16, 32, 768, 256], P('dp', None, 'lon')
- first_weight_gradient: float32 [589824], P(('lon', 'dp'))
- second_weight_gradient: float32 [589824], P(('lon', 'dp'))
All inputs are finite; a program needn't handle non-finite values.
Results may differ from a plain program's by a relative error of at most 0.0049.
Values may be sent and summed in bfloat16 or wider, within the bound.
A program may use at most 64 MiB of HBM per device.

v0:
```python
import jax
import jax.numpy as jnp
from jax import lax
from jax.experimental import pallas as pl
from jax.experimental.pallas import tpu as pltpu
from jax.sharding import PartitionSpec as P

BF = jnp.bfloat16
F32 = jnp.float32
LAT = 32
COLS = 48
CH = 256
HALF = 128
CELLS = LAT * COLS
LONS = 16
DPS = 16
ROWS = 9 * CH
BLOCK = ROWS // LONS
UNIT = BLOCK // DPS
PAD2 = 96
PAD1 = 64
W2 = 18
W1 = 12
M2 = 384
M1 = 256
MESH = pl.DeviceIdType.MESH
FAR_FIRST = sorted(range(1, DPS), key=lambda d: -min(d, DPS - d))
scope = jax.named_scope


def mm(a, b):
    return jnp.dot(a, b, preferred_element_type=F32)


def kernel(cot, pre2, x2, w1, w2, dx, g1, g2,
           V2, V1, S2, R2, S1, R1, pre, xin, w1b, w2b, wt1, wt2, hT, xT, acc, obuf,
           wf, wb, recvA, sY, sX, rY1, rX1, tY, tX, rY2, rX2, tYo, sC, sendD, recvD, gbuf,
           ld, st, hs, hr, as_, ar, ys, yr, xs, xr, ds_, dr, know1, know2):
    lon = lax.axis_index("lon")
    dp = lax.axis_index("dp")
    core = lax.rem(lon, 2)
    y = lax.rem(lax.div(lon, 2), 4)
    xh = lax.div(lon, 8)
    left = lax.rem(lon + LONS - 1, LONS)
    right = lax.rem(lon + 1, LONS)
    partner = lon + 1 - 2 * core
    ypeer = [lax.rem(y + d, 4) for d in range(1, 4)]
    ylon = [xh * 8 + yp * 2 + core for yp in ypeer]
    xlon = (1 - xh) * 8 + y * 2 + core
    dpeer = {d: lax.rem(dp + d, DPS) for d in range(1, DPS)}
    twin = dp + 1 - 2 * lax.rem(dp, 2)

    loads = []
    for i, (s, d) in enumerate((
        (cot, V2.at[1, PAD2:PAD2 + CELLS]), (w2, w2b), (pre2, pre), (x2, xin), (w1, w1b),
    )):
        c = pltpu.make_async_copy(s, d, ld.at[i])
        c.start()
        loads.append(c)

    barrier = pltpu.get_barrier_semaphore()

    def tell(sem, l, d):
        pl.semaphore_signal(sem, inc=1, device_id=(l, d), device_id_type=MESH)

    for l in [left, right, xlon] + ylon:
        tell(barrier, l, dp)
    for d in (dpeer[2], dpeer[14], dpeer[4], dpeer[12], twin):
        tell(barrier, lon, d)

    for c in range(3):
        V2[c, 0:PAD2] = jnp.zeros((PAD2, CH), BF)
        V2[c, PAD2 + CELLS:] = jnp.zeros((PAD2, CH), BF)
        V1[c, 0:PAD1] = jnp.zeros((PAD1, CH), BF)
        V1[c, PAD1 + CELLS:] = jnp.zeros((PAD1, CH), BF)
    for h in range(2):
        sC[h, BLOCK:] = jnp.zeros((16, HALF), F32)

    def remote(s, d, ss, rs, l, dd):
        c = pltpu.make_async_remote_copy(
            src_ref=s, dst_ref=d, send_sem=ss, recv_sem=rs,
            device_id=(l, dd), device_id_type=MESH)
        c.start()
        return c

    def wait_all(ref, sem):
        pltpu.make_async_copy(ref, ref, sem).wait()

    sent = []

    def pack(V, pad, S, w):
        for p in range(LAT):
            o = pad + p * COLS
            S[0, p * w:(p + 1) * w] = V[1, o + COLS - w:o + COLS]
            S[1, p * w:(p + 1) * w] = V[1, o:o + w]

    def build_inner(V, pad, w):
        for p in range(LAT):
            o = pad + p * COLS
            V[0, o:o + COLS - w] = V[1, o + w:o + COLS]
            V[2, o + w:o + COLS] = V[1, o:o + COLS - w]

    def build_edge(V, pad, R, w):
        for p in range(LAT):
            o = pad + p * COLS
            V[0, o + COLS - w:o + COLS] = R[1, p * w:(p + 1) * w]
            V[2, o:o + w] = R[0, p * w:(p + 1) * w]

    def send_halo(S, R, i):
        return [
            remote(S.at[0], R.at[0], hs.at[i], hr.at[i], right, dp),
            remote(S.at[1], R.at[1], hs.at[i + 1], hr.at[i + 1], left, dp),
        ]

    with scope("ld0"):
        loads[0].wait()
    with scope("pack2"):
        pack(V2, PAD2, S2, W2)
    with scope("barrier"):
        pl.semaphore_wait(barrier, 11)
    halo2 = send_halo(S2, R2, 0)
    for d in (dpeer[4], dpeer[12]):
        tell(know1, lon, d)
    with scope("inner2"):
        build_inner(V2, PAD2, W2)

    def tr_weights(w, wt):
        for c in range(3):
            for r in range(3):
                k = 3 * r + c
                wt[c, r * CH:(r + 1) * CH] = w[k * CH:(k + 1) * CH].T

    with scope("trans2"):
        loads[1].wait()
        tr_weights(w2b, wt2)
        loads[2].wait()
        for i in range(6):
            rows = pl.ds(i * CH, CH)
            hT[:, rows] = jnp.maximum(pre[rows], jnp.zeros((CH, CH), BF)).T

    blocks2 = ((0, 768, ((0, 960), (1, 96))), (768, 768, ((1, 864), (2, 0))))
    blocks1 = ((0, 512, ((0, 640), (1, 64))),
               (512, 512, ((0, 1152), (1, 576), (2, 0))),
               (1024, 512, ((1, 1088), (2, 512))))

    def dx_part(V, wt, cols, block, i, m):
        taps = block[2]
        lhs, rhs = [], []
        for c in cols:
            for r, s in taps:
                lhs.append(V[c, pl.ds(pl.multiple_of(s + i * m, 16), m)])
            rhs.append(wt[c, taps[0][0] * CH:(taps[-1][0] + 1) * CH])
        return mm(jnp.concatenate(lhs, axis=1), jnp.concatenate(rhs, axis=0))

    def dx_loop(V, wt, cols, blocks, m, put):
        for b in blocks:
            @pl.loop(0, b[1] // m)
            def _(i, b=b):
                put(pl.multiple_of(b[0] + i * m, m), dx_part(V, wt, cols, b, i, m))

    cells2 = ((0, 768, 960), (0, 1536, 96), (768, 768, 0))
    cells1 = ((0, 1024, 640), (0, 1536, 64), (512, 1024, 0))

    def dw(g, srcT, V, cells, cols):
        for c in cols:
            for r in range(3):
                a, n, s = cells[r]
                v = mm(srcT[:, a:a + n], V[c, s:s + n])
                k = 3 * r + c
                wf[g, k * CH:(k + 1) * CH] = v
                wb[g, k * CH:(k + 1) * CH] = v.astype(BF)

    def first2(m0, v):
        acc[pl.ds(m0, M2)] = v

    def mask2(m0, v):
        rows = pl.ds(m0, M2)
        lg = jnp.where(pre[rows].astype(F32) > 0, acc[rows] + v, 0.0).astype(BF)
        V1[1, pl.ds(pl.multiple_of(PAD1 + m0, 16), M2)] = lg

    def first1(m0, v):
        acc[pl.ds(m0, M1)] = v

    def last1(m0, v):
        rows = pl.ds(m0, M1)
        obuf[rows] = (acc[rows] + v).astype(BF)

    with scope("dx2c"):
        dx_loop(V2, wt2, (1,), blocks2, M2, first2)
    with scope("dw2c"):
        dw(1, hT, V2, cells2, (1,))
    with scope("know1"):
        pl.semaphore_wait(know1, 2)
        tell(know2, lon, twin)
    with scope("trans1"):
        loads[3].wait()
        for i in range(6):
            rows = pl.ds(i * CH, CH)
            xT[:, rows] = xin[rows].T
        loads[4].wait()
        tr_weights(w1b, wt1)

    with scope("halo2w"):
        for h in halo2:
            h.wait_recv()
    with scope("edge2"):
        build_edge(V2, PAD2, R2, W2)
    with scope("dx2lr"):
        dx_loop(V2, wt2, (0, 2), blocks2, M2, mask2)
    with scope("pack1"):
        pack(V1, PAD1, S1, W1)
    halo1 = send_halo(S1, R1, 2)
    with scope("dw2lr"):
        dw(1, hT, V2, cells2, (0, 2))

    def stage_a(g):
        for j in range(8):
            rows = pl.ds(pl.multiple_of((2 * j + 1 - core) * BLOCK, 16), BLOCK)
            remote(wb.at[g, rows], recvA.at[g, j], as_.at[g], ar.at[g], partner, dp)
        sent.append((recvA.at[g], as_.at[g]))

    def stage_b(g):
        wait_all(recvA.at[g], ar.at[g])

        @pl.loop(0, 8)
        def _(j):
            rows = pl.ds(pl.multiple_of((2 * j + core) * BLOCK, 16), BLOCK)
            v = (wf[g, rows] + recvA[g, j].astype(F32)).astype(BF)
            sY[g, lax.div(j, 4), lax.rem(j, 4)] = v[:, :HALF]
            sX[g, lax.div(j, 4), lax.rem(j, 4)] = v[:, HALF:]

        remote(sX.at[g, 1 - xh], rX1.at[g], xs.at[g, 0], xr.at[g, 0], xlon, dp)
        for d in (1, 0, 2):
            remote(sY.at[g, :, ypeer[d]], rY1.at[g, d], ys.at[g, 0], yr.at[g, 0], ylon[d], dp)
        sent.extend(((rX1.at[g], xs.at[g, 0]), (rY1.at[g], ys.at[g, 0])))

    def stage_cy(g):
        wait_all(rY1.at[g], yr.at[g, 0])
        for own, h in ((False, 1 - xh), (True, xh)):
            v = sY[g, h, y].astype(F32)
            for d in range(3):
                v = v + rY1[g, d, h].astype(F32)
            if own:
                tYo[g] = v
            else:
                tY[g] = v.astype(BF)
        remote(tY.at[g], rY2.at[g], xs.at[g, 1], xr.at[g, 1], xlon, dp)
        sent.append((rY2.at[g], xs.at[g, 1]))

    def stage_cx(g):
        wait_all(rX1.at[g], xr.at[g, 0])
        for i in range(4):
            tX[g, i] = (sX[g, xh, i].astype(F32) + rX1[g, i].astype(F32)).astype(BF)
        for d in (1, 0, 2):
            remote(tX.at[g, ypeer[d]], rX2.at[g, d], ys.at[g, 1], yr.at[g, 1], ylon[d], dp)
        sent.append((rX2.at[g], ys.at[g, 1]))

    def stage_d(g, h):
        if h == 0:
            wait_all(rY2.at[g], xr.at[g, 1])
            v = tYo[g] + rY2[g].astype(F32)
        else:
            wait_all(rX2.at[g], yr.at[g, 1])
            v = tX[g, y].astype(F32)
            for d in range(3):
                v = v + rX2[g, d].astype(F32)
        sC[h, 0:BLOCK] = v
        for u in range(DPS):
            sendD[g, h, u] = sC[h, u * UNIT:u * UNIT + 16].astype(BF)
        for d in FAR_FIRST:
            remote(sendD.at[g, h, dpeer[d]], recvD.at[g, h, d - 1],
                   ds_.at[g, h], dr.at[g, h], lon, dpeer[d])
        sent.append((recvD.at[g, h], ds_.at[g, h]))

    norm = float(16 * LAT * 768) ** -0.5

    def finish(g, h):
        wait_all(recvD.at[g, h], dr.at[g, h])
        v = sendD[g, h, dp].astype(F32)
        for d in range(DPS - 1):
            v = v + recvD[g, h, d].astype(F32)
        v = v * norm
        for u in range(UNIT):
            gbuf[g, pl.ds(u * CH + h * HALF, HALF)] = v[u]

    stage_a(1)
    with scope("inner1"):
        build_inner(V1, PAD1, W1)
    with scope("dx1c"):
        dx_loop(V1, wt1, (1,), blocks1, M1, first1)
    with scope("dw1c"):
        dw(0, xT, V1, cells1, (1,))
    with scope("halo1w"):
        for h in halo1:
            h.wait_recv()
    with scope("edge1"):
        build_edge(V1, PAD1, R1, W1)
    with scope("dw1lr"):
        dw(0, xT, V1, cells1, (0, 2))
    stage_a(0)
    with scope("b2"):
        stage_b(1)
    with scope("dx1lr"):
        dx_loop(V1, wt1, (0, 2), blocks1, M1, last1)
    store = pltpu.make_async_copy(obuf, dx, st.at[0])
    store.start()
    with scope("b1"):
        stage_b(0)
    with scope("c2y"):
        stage_cy(1)
    with scope("c2x"):
        stage_cx(1)
    with scope("c1y"):
        stage_cy(0)
    with scope("c1x"):
        stage_cx(0)
    with scope("know2"):
        pl.semaphore_wait(know2, 1)
    with scope("d2y"):
        stage_d(1, 0)
    with scope("d2x"):
        stage_d(1, 1)
    with scope("d1y"):
        stage_d(0, 0)
    with scope("d1x"):
        stage_d(0, 1)
    with scope("f2"):
        finish(1, 0)
        finish(1, 1)
        put2 = pltpu.make_async_copy(gbuf.at[1], g2, st.at[2])
        put2.start()
    with scope("f1"):
        finish(0, 0)
        finish(0, 1)
        put1 = pltpu.make_async_copy(gbuf.at[0], g1, st.at[1])
        put1.start()
    with scope("sends"):
        for c in halo2 + halo1:
            c.wait_send()
        for ref, sem in sent:
            wait_all(ref, sem)
        store.wait()
        put2.wait()
        put1.wait()


def write_out(dx, g1, g2, dxo, g1o, g2o, dxb, g1b, g2b, rd, wr):
    n = CELLS // 4
    parts = [(dx.at[i * n:(i + 1) * n], dxb.at[i * n:(i + 1) * n], dxo.at[i * n:(i + 1) * n])
             for i in range(4)] + [(g1, g1b, g1o), (g2, g2b, g2o)]
    ins = [pltpu.make_async_copy(s, b, rd.at[i]) for i, (s, b, _) in enumerate(parts)]
    outs = [pltpu.make_async_copy(b, d, wr.at[i]) for i, (_, b, d) in enumerate(parts)]
    for c in ins:
        c.start()
    for c, o in zip(ins, outs):
        c.wait()
        o.start()
    for o in outs:
        o.wait()


def local(inputs, pre_act, cotangent, first_weight, second_weight):
    hbm = pl.BlockSpec(memory_space=pltpu.HBM)
    any_ = pl.BlockSpec(memory_space=pl.ANY)
    V = pltpu.VMEM
    D = pltpu.SemaphoreType.DMA
    outs = (
        jax.ShapeDtypeStruct((CELLS, CH), BF),
        jax.ShapeDtypeStruct((UNIT * CH,), F32),
        jax.ShapeDtypeStruct((UNIT * CH,), F32),
    )
    got = pl.pallas_call(
        kernel,
        name="conv_back",
        out_shape=outs,
        in_specs=[hbm] * 5,
        out_specs=(any_,) * 3,
        scratch_shapes=[
            V((3, CELLS + 2 * PAD2, CH), BF), V((3, CELLS + 2 * PAD1, CH), BF),
            V((2, LAT * W2, CH), BF), V((2, LAT * W2, CH), BF),
            V((2, LAT * W1, CH), BF), V((2, LAT * W1, CH), BF),
            V((CELLS, CH), BF), V((CELLS, CH), BF),
            V((ROWS, CH), BF), V((ROWS, CH), BF),
            V((3, 3 * CH, CH), BF), V((3, 3 * CH, CH), BF),
            V((CH, CELLS), BF), V((CH, CELLS), BF),
            V((CELLS, CH), F32), V((CELLS, CH), BF),
            V((2, ROWS, CH), F32), V((2, ROWS, CH), BF),
            V((2, 8, BLOCK, CH), BF),
            V((2, 2, 4, BLOCK, HALF), BF), V((2, 2, 4, BLOCK, HALF), BF),
            V((2, 3, 2, BLOCK, HALF), BF), V((2, 4, BLOCK, HALF), BF),
            V((2, BLOCK, HALF), BF), V((2, 4, BLOCK, HALF), BF),
            V((2, BLOCK, HALF), BF), V((2, 3, BLOCK, HALF), BF),
            V((2, BLOCK, HALF), F32), V((2, BLOCK + 16, HALF), F32),
            V((2, 2, DPS, 16, HALF), BF), V((2, 2, DPS - 1, 16, HALF), BF), V((2, UNIT * CH), F32),
            D((5,)), D((3,)), D((4,)), D((4,)), D((2,)), D((2,)), D((2, 2)), D((2, 2)),
            D((2, 2)), D((2, 2)), D((2, 2)), D((2, 2)),
            pltpu.SemaphoreType.REGULAR, pltpu.SemaphoreType.REGULAR,
        ],
        compiler_params=pltpu.CompilerParams(
            collective_id=0, has_side_effects=True, vmem_limit_bytes=64300 * 1024),
    )(cotangent.reshape(CELLS, CH), pre_act.reshape(CELLS, CH), inputs.reshape(CELLS, CH),
      first_weight, second_weight)
    dx, g1, g2 = pl.pallas_call(
        write_out,
        name="write_out",
        out_shape=outs,
        in_specs=[any_] * 3,
        out_specs=(any_,) * 3,
        scratch_shapes=[V(o.shape, o.dtype) for o in outs] + [D((6,)), D((6,))],
        compiler_params=pltpu.CompilerParams(vmem_limit_bytes=64300 * 1024),
    )(*got)
    return dx.reshape(inputs.shape), g1, g2


def solution(mesh):
    whole = P("dp", None, "lon", None)
    return jax.shard_map(
        local, mesh=mesh, in_specs=(whole, whole, whole, P(), P()),
        out_specs=(whole, P(("lon", "dp")), P(("lon", "dp"))), check_vma=False)
```

profile of v0, /device:TPU:2, one launch (start us, length us, event | category | flops | bytes accessed | tf_op | source)
XLA Modules:
  0.0 45.8 jit_solution(6477443904313232958)
XLA Ops:
  0.6 43.1 %conv_back.1 = (bf16[1536,256]{1,0:T(8,128)(2,1)}, f32[2304]{0:T(1024)}, f32[2304]{0:T(1024)}) custom-call(bf16[1536,256]{1,0:T(8,128)(2,1)} %bitcast.4, bf16[1536,256]{1,0:T(8,128)(2,1)} %bitcast.5, bf16[1536,256]{1,0:T(8,128)(2,1)} %bitcast.6, bf16[2304,256]{1,0:T(8,128)(2,1)} %w1.1, bf16[2304,256]{1,0:T(8,128)(2,1)} %w2.1), custom_call_target="tpu_custom_call" | custom-call | tf_op jit(solution)/shard_map/conv_back/pallas_call | solution.py:372
  43.8 2.0 %write_out.1 = (bf16[1536,256]{1,0:T(8,128)(2,1)}, f32[2304]{0:T(1024)}, f32[2304]{0:T(1024)}) custom-call(bf16[1536,256]{1,0:T(8,128)(2,1)} %get-tuple-element.9.dx, f32[2304]{0:T(1024)} %get-tuple-element.10.g1, f32[2304]{0:T(1024)} %get-tuple-element.11.g2), custom_call_target="tpu_custom_call" | custom-call | tf_op jit(solution)/shard_map/write_out/pallas_call | solution.py:403
where the time goes:
time: 45.9 us; the launch traced here: 45.8 us
  Pallas kernels  45.1 us (98%)
  between operations  0.64 us (1%)
    pallas_call x1, Pallas kernels, local(): pl.pallas_call(kernel, name='conv_back', out_shape=outs, in_specs=[hbm] *...  43.1 us
    pallas_call x1, Pallas kernels, local(): pl.pallas_call(write_out, name='write_out', out_shape=outs, in_specs=[any...  2 us

commit v1 on v0

--- a/solution.py
+++ b/solution.py
@@ -18,6 +18,8 @@
 BLOCK = ROWS // LONS
 UNIT = BLOCK // DPS
 PAD2 = 96
+TOP = 80
+REST = BLOCK - TOP
 PAD1 = 64
 W2 = 18
 W1 = 12
@@ -34,7 +36,7 @@
 
 def kernel(cot, pre2, x2, w1, w2, dx, g1, g2,
            V2, V1, S2, R2, S1, R1, pre, xin, w1b, w2b, wt1, wt2, hT, xT, acc, obuf,
-           wf, wb, recvA, sY, sX, rY1, rX1, tY, tX, rY2, rX2, tYo, sC, sendD, recvD, gbuf,
+           wf, wb, recvA, sY, sX, rY1, rX1, tY, tX, rY2, rX2, sC, sendD, recvD, gbuf,
            ld, st, hs, hr, as_, ar, ys, yr, xs, xr, ds_, dr, know1, know2):
     lon = lax.axis_index("lon")
     dp = lax.axis_index("dp")
@@ -46,7 +48,10 @@
     partner = lon + 1 - 2 * core
     ypeer = [lax.rem(y + d, 4) for d in range(1, 4)]
     ylon = [xh * 8 + yp * 2 + core for yp in ypeer]
-    xlon = (1 - xh) * 8 + y * 2 + core
+    xl = lax.rem(dp, 2)
+    xat = [lax.rem(2 * xh + xl + e, 4) for e in range(1, 4)]
+    xpeer = [(lax.div(a, 2), lax.rem(a, 2)) for a in xat]
+    xid = [(h * 8 + y * 2 + core, dp - xl + l) for h, l in xpeer]
     dpeer = {d: lax.rem(dp + d, DPS) for d in range(1, DPS)}
     twin = dp + 1 - 2 * lax.rem(dp, 2)
 
@@ -63,9 +68,11 @@
     def tell(sem, l, d):
         pl.semaphore_signal(sem, inc=1, device_id=(l, d), device_id_type=MESH)
 
-    for l in [left, right, xlon] + ylon:
+    for l in [left, right] + ylon:
         tell(barrier, l, dp)
-    for d in (dpeer[2], dpeer[14], dpeer[4], dpeer[12], twin):
+    for l, d in xid:
+        tell(barrier, l, d)
+    for d in (dpeer[2], dpeer[14], dpeer[4], dpeer[12]):
         tell(barrier, lon, d)
 
     for c in range(3):
@@ -73,8 +80,7 @@
         V2[c, PAD2 + CELLS:] = jnp.zeros((PAD2, CH), BF)
         V1[c, 0:PAD1] = jnp.zeros((PAD1, CH), BF)
         V1[c, PAD1 + CELLS:] = jnp.zeros((PAD1, CH), BF)
-    for h in range(2):
-        sC[h, BLOCK:] = jnp.zeros((16, HALF), F32)
+    sC[BLOCK:] = jnp.zeros((16, HALF), F32)
 
     def remote(s, d, ss, rs, l, dd):
         c = pltpu.make_async_remote_copy(
@@ -100,11 +106,22 @@
             V[0, o:o + COLS - w] = V[1, o + w:o + COLS]
             V[2, o + w:o + COLS] = V[1, o:o + COLS - w]
 
-    def build_edge(V, pad, R, w):
-        for p in range(LAT):
-            o = pad + p * COLS
-            V[0, o + COLS - w:o + COLS] = R[1, p * w:(p + 1) * w]
-            V[2, o:o + w] = R[0, p * w:(p + 1) * w]
+    early, late = 2 * core, 2 - 2 * core
+
+    def build_edge(V, pad, R, w, i, first):
+        wait_all(R.at[1 - core if first else core], hr.at[i + 1 - core if first else i + core])
+
+        @pl.when(core == (0 if first else 1))
+        def _():
+            for p in range(LAT):
+                o = pad + p * COLS
+                V[0, o + COLS - w:o + COLS] = R[1, p * w:(p + 1) * w]
+
+        @pl.when(core == (1 if first else 0))
+        def _():
+            for p in range(LAT):
+                o = pad + p * COLS
+                V[2, o:o + w] = R[0, p * w:(p + 1) * w]
 
     def send_halo(S, R, i):
         return [
@@ -117,7 +134,7 @@
     with scope("pack2"):
         pack(V2, PAD2, S2, W2)
     with scope("barrier"):
-        pl.semaphore_wait(barrier, 11)
+        pl.semaphore_wait(barrier, 12)
     halo2 = send_halo(S2, R2, 0)
     for d in (dpeer[4], dpeer[12]):
         tell(know1, lon, d)
@@ -166,12 +183,15 @@
             for r in range(3):
                 a, n, s = cells[r]
                 v = mm(srcT[:, a:a + n], V[c, s:s + n])
-                k = 3 * r + c
-                wf[g, k * CH:(k + 1) * CH] = v
-                wb[g, k * CH:(k + 1) * CH] = v.astype(BF)
+                rows = pl.ds(pl.multiple_of((3 * r + c) * CH, CH), CH)
+                wf[g, rows] = v
+                wb[g, rows] = v.astype(BF)
 
     def first2(m0, v):
         acc[pl.ds(m0, M2)] = v
+
+    def more2(m0, v):
+        acc[pl.ds(m0, M2)] += v
 
     def mask2(m0, v):
         rows = pl.ds(m0, M2)
@@ -180,6 +200,9 @@
 
     def first1(m0, v):
         acc[pl.ds(m0, M1)] = v
+
+    def more1(m0, v):
+        acc[pl.ds(m0, M1)] += v
 
     def last1(m0, v):
         rows = pl.ds(m0, M1)
@@ -200,18 +223,21 @@
         loads[4].wait()
         tr_weights(w1b, wt1)
 
-    with scope("halo2w"):
-        for h in halo2:
-            h.wait_recv()
-    with scope("edge2"):
-        build_edge(V2, PAD2, R2, W2)
-    with scope("dx2lr"):
-        dx_loop(V2, wt2, (0, 2), blocks2, M2, mask2)
+    with scope("halo2e"):
+        build_edge(V2, PAD2, R2, W2, 0, True)
+    with scope("dx2e"):
+        dx_loop(V2, wt2, (early,), blocks2, M2, more2)
+    with scope("dw2e"):
+        dw(1, hT, V2, cells2, (early,))
+    with scope("halo2l"):
+        build_edge(V2, PAD2, R2, W2, 0, False)
+    with scope("dx2l"):
+        dx_loop(V2, wt2, (late,), blocks2, M2, mask2)
     with scope("pack1"):
         pack(V1, PAD1, S1, W1)
     halo1 = send_halo(S1, R1, 2)
-    with scope("dw2lr"):
-        dw(1, hT, V2, cells2, (0, 2))
+    with scope("dw2l"):
+        dw(1, hT, V2, cells2, (late,))
 
     def stage_a(g):
         for j in range(8):
@@ -226,62 +252,74 @@
         def _(j):
             rows = pl.ds(pl.multiple_of((2 * j + core) * BLOCK, 16), BLOCK)
             v = (wf[g, rows] + recvA[g, j].astype(F32)).astype(BF)
-            sY[g, lax.div(j, 4), lax.rem(j, 4)] = v[:, :HALF]
-            sX[g, lax.div(j, 4), lax.rem(j, 4)] = v[:, HALF:]
-
-        remote(sX.at[g, 1 - xh], rX1.at[g], xs.at[g, 0], xr.at[g, 0], xlon, dp)
+            h, yy = lax.div(j, 4), lax.rem(j, 4)
+            sY[g, h, yy] = v[:TOP]
+            sX[g, h, 0, yy] = v[TOP:, :HALF]
+            sX[g, h, 1, yy] = v[TOP:, HALF:]
+
+        for e in (1, 0, 2):
+            h, l = xpeer[e]
+            remote(sX.at[g, h, l], rX1.at[g, e], xs.at[g, 0], xr.at[g, 0], *xid[e])
         for d in (1, 0, 2):
             remote(sY.at[g, :, ypeer[d]], rY1.at[g, d], ys.at[g, 0], yr.at[g, 0], ylon[d], dp)
         sent.extend(((rX1.at[g], xs.at[g, 0]), (rY1.at[g], ys.at[g, 0])))
 
     def stage_cy(g):
         wait_all(rY1.at[g], yr.at[g, 0])
-        for own, h in ((False, 1 - xh), (True, xh)):
+        for h in range(2):
             v = sY[g, h, y].astype(F32)
             for d in range(3):
                 v = v + rY1[g, d, h].astype(F32)
-            if own:
-                tYo[g] = v
-            else:
-                tY[g] = v.astype(BF)
-        remote(tY.at[g], rY2.at[g], xs.at[g, 1], xr.at[g, 1], xlon, dp)
+            v = v.astype(BF)
+            tY[g, h, 0] = v[:, :HALF]
+            tY[g, h, 1] = v[:, HALF:]
+        for e in (1, 0, 2):
+            h, l = xpeer[e]
+            remote(tY.at[g, h, l], rY2.at[g, e], xs.at[g, 1], xr.at[g, 1], *xid[e])
         sent.append((rY2.at[g], xs.at[g, 1]))
 
     def stage_cx(g):
         wait_all(rX1.at[g], xr.at[g, 0])
         for i in range(4):
-            tX[g, i] = (sX[g, xh, i].astype(F32) + rX1[g, i].astype(F32)).astype(BF)
+            v = sX[g, xh, xl, i].astype(F32)
+            for e in range(3):
+                v = v + rX1[g, e, i].astype(F32)
+            tX[g, i] = v.astype(BF)
         for d in (1, 0, 2):
             remote(tX.at[g, ypeer[d]], rX2.at[g, d], ys.at[g, 1], yr.at[g, 1], ylon[d], dp)
         sent.append((rX2.at[g], ys.at[g, 1]))
 
-    def stage_d(g, h):
-        if h == 0:
-            wait_all(rY2.at[g], xr.at[g, 1])
-            v = tYo[g] + rY2[g].astype(F32)
-        else:
-            wait_all(rX2.at[g], yr.at[g, 1])
-            v = tX[g, y].astype(F32)
-            for d in range(3):
-                v = v + rX2[g, d].astype(F32)
-        sC[h, 0:BLOCK] = v
+    def stage_d(g):
+        wait_all(rY2.at[g], xr.at[g, 1])
+        v = tY[g, xh, xl].astype(F32)
+        for e in range(3):
+            v = v + rY2[g, e].astype(F32)
+        sC[0:TOP] = v
+        wait_all(rX2.at[g], yr.at[g, 1])
+        v = tX[g, y].astype(F32)
+        for d in range(3):
+            v = v + rX2[g, d].astype(F32)
+        sC[TOP:BLOCK] = v
         for u in range(DPS):
-            sendD[g, h, u] = sC[h, u * UNIT:u * UNIT + 16].astype(BF)
+            sendD[g, u] = sC[u * UNIT:u * UNIT + 16].astype(BF)
         for d in FAR_FIRST:
-            remote(sendD.at[g, h, dpeer[d]], recvD.at[g, h, d - 1],
-                   ds_.at[g, h], dr.at[g, h], lon, dpeer[d])
-        sent.append((recvD.at[g, h], ds_.at[g, h]))
+            remote(sendD.at[g, dpeer[d]], recvD.at[g, d - 1], ds_.at[g], dr.at[g], lon, dpeer[d])
+        sent.append((recvD.at[g], ds_.at[g]))
 
     norm = float(16 * LAT * 768) ** -0.5
 
-    def finish(g, h):
-        wait_all(recvD.at[g, h], dr.at[g, h])
-        v = sendD[g, h, dp].astype(F32)
-        for d in range(DPS - 1):
-            v = v + recvD[g, h, d].astype(F32)
-        v = v * norm
-        for u in range(UNIT):
-            gbuf[g, pl.ds(u * CH + h * HALF, HALF)] = v[u]
+    def finish(g):
+        wait_all(recvD.at[g], dr.at[g])
+        mine = sendD[g, dp].astype(F32)
+        for d in range(2, DPS, 2):
+            mine = mine + recvD[g, d - 1].astype(F32)
+        other = recvD[g, 0].astype(F32)
+        for d in range(3, DPS, 2):
+            other = other + recvD[g, d - 1].astype(F32)
+        for h, v in enumerate((jnp.where(xl == 0, mine, other), jnp.where(xl == 0, other, mine))):
+            v = v * norm
+            for u in range(UNIT):
+                gbuf[g, pl.ds(u * CH + h * HALF, HALF)] = v[u]
 
     stage_a(1)
     with scope("inner1"):
@@ -290,18 +328,21 @@
         dx_loop(V1, wt1, (1,), blocks1, M1, first1)
     with scope("dw1c"):
         dw(0, xT, V1, cells1, (1,))
-    with scope("halo1w"):
-        for h in halo1:
-            h.wait_recv()
-    with scope("edge1"):
-        build_edge(V1, PAD1, R1, W1)
-    with scope("dw1lr"):
-        dw(0, xT, V1, cells1, (0, 2))
+    with scope("halo1e"):
+        build_edge(V1, PAD1, R1, W1, 2, True)
+    with scope("dw1e"):
+        dw(0, xT, V1, cells1, (early,))
+    with scope("dx1e"):
+        dx_loop(V1, wt1, (early,), blocks1, M1, more1)
+    with scope("halo1l"):
+        build_edge(V1, PAD1, R1, W1, 2, False)
+    with scope("dw1l"):
+        dw(0, xT, V1, cells1, (late,))
     stage_a(0)
     with scope("b2"):
         stage_b(1)
-    with scope("dx1lr"):
-        dx_loop(V1, wt1, (0, 2), blocks1, M1, last1)
+    with scope("dx1l"):
+        dx_loop(V1, wt1, (late,), blocks1, M1, last1)
     store = pltpu.make_async_copy(obuf, dx, st.at[0])
     store.start()
     with scope("b1"):
@@ -316,22 +357,16 @@
         stage_cx(0)
     with scope("know2"):
         pl.semaphore_wait(know2, 1)
-    with scope("d2y"):
-        stage_d(1, 0)
-    with scope("d2x"):
-        stage_d(1, 1)
-    with scope("d1y"):
-        stage_d(0, 0)
-    with scope("d1x"):
-        stage_d(0, 1)
+    with scope("d2"):
+        stage_d(1)
+    with scope("d1"):
+        stage_d(0)
     with scope("f2"):
-        finish(1, 0)
-        finish(1, 1)
+        finish(1)
         put2 = pltpu.make_async_copy(gbuf.at[1], g2, st.at[2])
         put2.start()
     with scope("f1"):
-        finish(0, 0)
-        finish(0, 1)
+        finish(0)
         put1 = pltpu.make_async_copy(gbuf.at[0], g1, st.at[1])
         put1.start()
     with scope("sends"):
@@ -386,14 +421,14 @@
             V((CELLS, CH), F32), V((CELLS, CH), BF),
             V((2, ROWS, CH), F32), V((2, ROWS, CH), BF),
             V((2, 8, BLOCK, CH), BF),
-            V((2, 2, 4, BLOCK, HALF), BF), V((2, 2, 4, BLOCK, HALF), BF),
-            V((2, 3, 2, BLOCK, HALF), BF), V((2, 4, BLOCK, HALF), BF),
-            V((2, BLOCK, HALF), BF), V((2, 4, BLOCK, HALF), BF),
-            V((2, BLOCK, HALF), BF), V((2, 3, BLOCK, HALF), BF),
-            V((2, BLOCK, HALF), F32), V((2, BLOCK + 16, HALF), F32),
-            V((2, 2, DPS, 16, HALF), BF), V((2, 2, DPS - 1, 16, HALF), BF), V((2, UNIT * CH), F32),
+            V((2, 2, 4, TOP, CH), BF), V((2, 2, 2, 4, REST, HALF), BF),
+            V((2, 3, 2, TOP, CH), BF), V((2, 3, 4, REST, HALF), BF),
+            V((2, 2, 2, TOP, HALF), BF), V((2, 4, REST, HALF), BF),
+            V((2, 3, TOP, HALF), BF), V((2, 3, REST, HALF), BF),
+            V((BLOCK + 16, HALF), F32),
+            V((2, DPS, 16, HALF), BF), V((2, DPS - 1, 16, HALF), BF), V((2, UNIT * CH), F32),
             D((5,)), D((3,)), D((4,)), D((4,)), D((2,)), D((2,)), D((2, 2)), D((2, 2)),
-            D((2, 2)), D((2, 2)), D((2, 2)), D((2, 2)),
+            D((2, 2)), D((2, 2)), D((2,)), D((2,)),
             pltpu.SemaphoreType.REGULAR, pltpu.SemaphoreType.REGULAR,
         ],
         compiler_params=pltpu.CompilerParams(

time: 45.9 us -> 44.3 us (0.965)
  Pallas kernels: 45.1 us -> 43.3 us
    pallas_call x1, Pallas kernels: 43.1 us -> 41.3 us  [local(): pl.pallas_call(kernel, name='conv_back', out_shape=outs, in_specs=[hbm] *...]
where the time goes in v1:
time: 44.3 us; the launch traced here: 43.9 us
  Pallas kernels  43.3 us (98%)
  between operations  0.64 us (1%)
    pallas_call x1, Pallas kernels, local(): pl.pallas_call(kernel, name='conv_back', out_shape=outs, in_specs=[hbm] *...  41.3 us
    pallas_call x1, Pallas kernels, local(): pl.pallas_call(write_out, name='write_out', out_shape=outs, in_specs=[any...  2 us

profile of v1, /device:TPU:2, one launch (start us, length us, event | category | flops | bytes accessed | tf_op | source)
XLA Modules:
  0.0 43.9 jit_solution(12820318050947558493)
XLA Ops:
  0.6 41.3 %conv_back.1 = (bf16[1536,256]{1,0:T(8,128)(2,1)}, f32[2304]{0:T(1024)}, f32[2304]{0:T(1024)}) custom-call(bf16[1536,256]{1,0:T(8,128)(2,1)} %bitcast.4, bf16[1536,256]{1,0:T(8,128)(2,1)} %bitcast.5, bf16[1536,256]{1,0:T(8,128)(2,1)} %bitcast.6, bf16[2304,256]{1,0:T(8,128)(2,1)} %w1.1, bf16[2304,256]{1,0:T(8,128)(2,1)} %w2.1), custom_call_target="tpu_custom_call" | custom-call | tf_op jit(solution)/shard_map/conv_back/pallas_call | solution.py:407
  41.9 2.0 %write_out.1 = (bf16[1536,256]{1,0:T(8,128)(2,1)}, f32[2304]{0:T(1024)}, f32[2304]{0:T(1024)}) custom-call(bf16[1536,256]{1,0:T(8,128)(2,1)} %get-tuple-element.9.dx, f32[2304]{0:T(1024)} %get-tuple-element.10.g1, f32[2304]{0:T(1024)} %get-tuple-element.11.g2), custom_call_target="tpu_custom_call" | custom-call | tf_op jit(solution)/shard_map/write_out/pallas_call | solution.py:438

commit v2 on v1

--- a/solution.py
+++ b/solution.py
@@ -35,9 +35,9 @@
 
 
 def kernel(cot, pre2, x2, w1, w2, dx, g1, g2,
-           V2, V1, S2, R2, S1, R1, pre, xin, w1b, w2b, wt1, wt2, hT, xT, acc, obuf,
-           wf, wb, recvA, sY, sX, rY1, rX1, tY, tX, rY2, rX2, sC, sendD, recvD, gbuf,
-           ld, st, hs, hr, as_, ar, ys, yr, xs, xr, ds_, dr, know1, know2):
+           V2, V1, S2, R2, S1, R1, pre, xin, w1b, w2b, wt1, wt2, hT, xT, acc,
+           wf, wb, recvA, sY, sX, rY1, rX1, tY, tX, rY2, rX2, sC, sendD, recvD,
+           ld, hs, hr, as_, ar, ys, yr, xs, xr, ds_, dr, know1, know2):
     lon = lax.axis_index("lon")
     dp = lax.axis_index("dp")
     core = lax.rem(lon, 2)
@@ -206,7 +206,7 @@
 
     def last1(m0, v):
         rows = pl.ds(m0, M1)
-        obuf[rows] = (acc[rows] + v).astype(BF)
+        dx[rows] = (acc[rows] + v).astype(BF)
 
     with scope("dx2c"):
         dx_loop(V2, wt2, (1,), blocks2, M2, first2)
@@ -308,7 +308,7 @@
 
     norm = float(16 * LAT * 768) ** -0.5
 
-    def finish(g):
+    def finish(g, out):
         wait_all(recvD.at[g], dr.at[g])
         mine = sendD[g, dp].astype(F32)
         for d in range(2, DPS, 2):
@@ -319,7 +319,7 @@
         for h, v in enumerate((jnp.where(xl == 0, mine, other), jnp.where(xl == 0, other, mine))):
             v = v * norm
             for u in range(UNIT):
-                gbuf[g, pl.ds(u * CH + h * HALF, HALF)] = v[u]
+                out[pl.ds(u * CH + h * HALF, HALF)] = v[u]
 
     stage_a(1)
     with scope("inner1"):
@@ -343,8 +343,6 @@
         stage_b(1)
     with scope("dx1l"):
         dx_loop(V1, wt1, (late,), blocks1, M1, last1)
-    store = pltpu.make_async_copy(obuf, dx, st.at[0])
-    store.start()
     with scope("b1"):
         stage_b(0)
     with scope("c2y"):
@@ -362,40 +360,28 @@
     with scope("d1"):
         stage_d(0)
     with scope("f2"):
-        finish(1)
-        put2 = pltpu.make_async_copy(gbuf.at[1], g2, st.at[2])
-        put2.start()
+        finish(1, g2)
     with scope("f1"):
-        finish(0)
-        put1 = pltpu.make_async_copy(gbuf.at[0], g1, st.at[1])
-        put1.start()
+        finish(0, g1)
     with scope("sends"):
         for c in halo2 + halo1:
             c.wait_send()
         for ref, sem in sent:
             wait_all(ref, sem)
-        store.wait()
-        put2.wait()
-        put1.wait()
-
-
-def write_out(dx, g1, g2, dxo, g1o, g2o, dxb, g1b, g2b, rd, wr):
-    n = CELLS // 4
-    parts = [(dx.at[i * n:(i + 1) * n], dxb.at[i * n:(i + 1) * n], dxo.at[i * n:(i + 1) * n])
-             for i in range(4)] + [(g1, g1b, g1o), (g2, g2b, g2o)]
-    ins = [pltpu.make_async_copy(s, b, rd.at[i]) for i, (s, b, _) in enumerate(parts)]
-    outs = [pltpu.make_async_copy(b, d, wr.at[i]) for i, (_, b, d) in enumerate(parts)]
-    for c in ins:
+
+
+def write_out(dx, g1, g2, dxo, g1o, g2o, sem):
+    copies = [pltpu.make_async_copy(s, d, sem.at[i])
+              for i, (s, d) in enumerate(((g1, g1o), (g2, g2o), (dx, dxo)))]
+    for c in copies:
         c.start()
-    for c, o in zip(ins, outs):
+    for c in copies:
         c.wait()
-        o.start()
-    for o in outs:
-        o.wait()
 
 
 def local(inputs, pre_act, cotangent, first_weight, second_weight):
     hbm = pl.BlockSpec(memory_space=pltpu.HBM)
+    vm = pl.BlockSpec(memory_space=pltpu.VMEM)
     any_ = pl.BlockSpec(memory_space=pl.ANY)
     V = pltpu.VMEM
     D = pltpu.SemaphoreType.DMA
@@ -409,7 +395,7 @@
         name="conv_back",
         out_shape=outs,
         in_specs=[hbm] * 5,
-        out_specs=(any_,) * 3,
+        out_specs=(vm,) * 3,
         scratch_shapes=[
             V((3, CELLS + 2 * PAD2, CH), BF), V((3, CELLS + 2 * PAD1, CH), BF),
             V((2, LAT * W2, CH), BF), V((2, LAT * W2, CH), BF),
@@ -418,7 +404,7 @@
             V((ROWS, CH), BF), V((ROWS, CH), BF),
             V((3, 3 * CH, CH), BF), V((3, 3 * CH, CH), BF),
             V((CH, CELLS), BF), V((CH, CELLS), BF),
-            V((CELLS, CH), F32), V((CELLS, CH), BF),
+            V((CELLS, CH), F32),
             V((2, ROWS, CH), F32), V((2, ROWS, CH), BF),
             V((2, 8, BLOCK, CH), BF),
             V((2, 2, 4, TOP, CH), BF), V((2, 2, 2, 4, REST, HALF), BF),
@@ -426,23 +412,23 @@
             V((2, 2, 2, TOP, HALF), BF), V((2, 4, REST, HALF), BF),
             V((2, 3, TOP, HALF), BF), V((2, 3, REST, HALF), BF),
             V((BLOCK + 16, HALF), F32),
-            V((2, DPS, 16, HALF), BF), V((2, DPS - 1, 16, HALF), BF), V((2, UNIT * CH), F32),
-            D((5,)), D((3,)), D((4,)), D((4,)), D((2,)), D((2,)), D((2, 2)), D((2, 2)),
+            V((2, DPS, 16, HALF), BF), V((2, DPS - 1, 16, HALF), BF),
+            D((5,)), D((4,)), D((4,)), D((2,)), D((2,)), D((2, 2)), D((2, 2)),
             D((2, 2)), D((2, 2)), D((2,)), D((2,)),
             pltpu.SemaphoreType.REGULAR, pltpu.SemaphoreType.REGULAR,
         ],
         compiler_params=pltpu.CompilerParams(
-            collective_id=0, has_side_effects=True, vmem_limit_bytes=64300 * 1024),
+            collective_id=0, has_side_effects=True, vmem_limit_bytes=53760 * 1024),
     )(cotangent.reshape(CELLS, CH), pre_act.reshape(CELLS, CH), inputs.reshape(CELLS, CH),
       first_weight, second_weight)
     dx, g1, g2 = pl.pallas_call(
         write_out,
         name="write_out",
         out_shape=outs,
-        in_specs=[any_] * 3,
+        in_specs=[vm] * 3,
         out_specs=(any_,) * 3,
-        scratch_shapes=[V(o.shape, o.dtype) for o in outs] + [D((6,)), D((6,))],
-        compiler_params=pltpu.CompilerParams(vmem_limit_bytes=64300 * 1024),
+        scratch_shapes=[D((3,))],
+        compiler_params=pltpu.CompilerParams(vmem_limit_bytes=1024 * 1024),
     )(*got)
     return dx.reshape(inputs.shape), g1, g2
 

time: 44.3 us -> 42.5 us (0.959)
  Pallas kernels: 43.3 us -> 41.6 us
    pallas_call x1, Pallas kernels: 2 us -> 0.92 us  [local(): pl.pallas_call(write_out, name='write_out', out_shape=outs, in_specs=[vm]...]
    pallas_call x1, Pallas kernels: 41.3 us -> 40.7 us  [local(): pl.pallas_call(kernel, name='conv_back', out_shape=outs, in_specs=[hbm] *...]
where the time goes in v2:
time: 42.5 us; the launch traced here: 42.3 us
  Pallas kernels  41.6 us (98%)
  between operations  0.64 us (2%)
    pallas_call x1, Pallas kernels, local(): pl.pallas_call(kernel, name='conv_back', out_shape=outs, in_specs=[hbm] *...  40.7 us
    pallas_call x1, Pallas kernels, local(): pl.pallas_call(write_out, name='write_out', out_shape=outs, in_specs=[vm]...  0.92 us

profile of v2, /device:TPU:2, one launch (start us, length us, event | category | flops | bytes accessed | tf_op | source)
XLA Modules:
  0.0 42.3 jit_solution(774046610677637536)
XLA Ops:
  0.6 40.7 %conv_back.1 = (bf16[1536,256]{1,0:T(8,128)(2,1)S(1)}, f32[2304]{0:T(1024)S(1)}, f32[2304]{0:T(1024)S(1)}) custom-call(bf16[1536,256]{1,0:T(8,128)(2,1)} %bitcast.4, bf16[1536,256]{1,0:T(8,128)(2,1)} %bitcast.5, bf16[1536,256]{1,0:T(8,128)(2,1)} %bitcast.6, bf16[2304,256]{1,0:T(8,128)(2,1)} %w1.1, bf16[2304,256]{1,0:T(8,128)(2,1)} %w2.1), custom_call_target="tpu_custom_call" | custom-call | tf_op jit(solution)/shard_map/conv_back/pallas_call | solution.py:393
  41.3 0.9 %write_out.1 = (bf16[1536,256]{1,0:T(8,128)(2,1)}, f32[2304]{0:T(1024)}, f32[2304]{0:T(1024)}) custom-call(bf16[1536,256]{1,0:T(8,128)(2,1)S(1)} %get-tuple-element.9.dx, f32[2304]{0:T(1024)S(1)} %get-tuple-element.10.g1, f32[2304]{0:T(1024)S(1)} %get-tuple-element.11.g2), custom_call_target="tpu_custom_call" | custom-call | tf_op jit(solution)/shard_map/write_out/pallas_call | solution.py:424

commit v3 on v2

--- a/solution.py
+++ b/solution.py
@@ -18,7 +18,7 @@
 BLOCK = ROWS // LONS
 UNIT = BLOCK // DPS
 PAD2 = 96
-TOP = 80
+TOP = 64
 REST = BLOCK - TOP
 PAD1 = 64
 W2 = 18
@@ -94,8 +94,10 @@
 
     sent = []
 
-    def pack(V, pad, S, w):
-        for p in range(LAT):
+    halves = (range(0, LAT // 2), range(LAT // 2, LAT))
+
+    def pack(V, pad, S, w, lats=range(LAT)):
+        for p in lats:
             o = pad + p * COLS
             S[0, p * w:(p + 1) * w] = V[1, o + COLS - w:o + COLS]
             S[1, p * w:(p + 1) * w] = V[1, o:o + w]
@@ -108,26 +110,30 @@
 
     early, late = 2 * core, 2 - 2 * core
 
-    def build_edge(V, pad, R, w, i, first):
-        wait_all(R.at[1 - core if first else core], hr.at[i + 1 - core if first else i + core])
+    def build_edge(V, pad, R, w, i, first, q):
+        n = LAT // 2 * w
+        wait_all(R.at[1 - core if first else core, q * n:(q + 1) * n],
+                 hr.at[i, 1 - core if first else core, q])
 
         @pl.when(core == (0 if first else 1))
         def _():
-            for p in range(LAT):
+            for p in halves[q]:
                 o = pad + p * COLS
                 V[0, o + COLS - w:o + COLS] = R[1, p * w:(p + 1) * w]
 
         @pl.when(core == (1 if first else 0))
         def _():
-            for p in range(LAT):
+            for p in halves[q]:
                 o = pad + p * COLS
                 V[2, o:o + w] = R[0, p * w:(p + 1) * w]
 
-    def send_halo(S, R, i):
-        return [
-            remote(S.at[0], R.at[0], hs.at[i], hr.at[i], right, dp),
-            remote(S.at[1], R.at[1], hs.at[i + 1], hr.at[i + 1], left, dp),
-        ]
+    def send_halo(S, R, i, q):
+        n = S.shape[1] // 2
+        rows = slice(q * n, (q + 1) * n)
+        remote(S.at[0, rows], R.at[0, rows], hs.at[i, 0], hr.at[i, 0, q], right, dp)
+        remote(S.at[1, rows], R.at[1, rows], hs.at[i, 1], hr.at[i, 1, q], left, dp)
+        if q:
+            sent.extend(((R.at[0], hs.at[i, 0]), (R.at[1], hs.at[i, 1])))
 
     with scope("ld0"):
         loads[0].wait()
@@ -135,7 +141,8 @@
         pack(V2, PAD2, S2, W2)
     with scope("barrier"):
         pl.semaphore_wait(barrier, 12)
-    halo2 = send_halo(S2, R2, 0)
+    for q in range(2):
+        send_halo(S2, R2, 0, q)
     for d in (dpeer[4], dpeer[12]):
         tell(know1, lon, d)
     with scope("inner2"):
@@ -187,6 +194,16 @@
                 wf[g, rows] = v
                 wb[g, rows] = v.astype(BF)
 
+    def dw_part(cells, last):
+        for r in range(3):
+            a, n, s = cells[r]
+            v = mm(xT[:, a:a + n], V1[late, s:s + n])
+            rows = pl.ds(pl.multiple_of((3 * r + late) * CH, CH), CH)
+            if last:
+                v = v + wf[0, rows]
+                wb[0, rows] = v.astype(BF)
+            wf[0, rows] = v
+
     def first2(m0, v):
         acc[pl.ds(m0, M2)] = v
 
@@ -203,6 +220,9 @@
 
     def more1(m0, v):
         acc[pl.ds(m0, M1)] += v
+
+    def only1(m0, v):
+        dx[pl.ds(m0, M1)] = v.astype(BF)
 
     def last1(m0, v):
         rows = pl.ds(m0, M1)
@@ -224,18 +244,24 @@
         tr_weights(w1b, wt1)
 
     with scope("halo2e"):
-        build_edge(V2, PAD2, R2, W2, 0, True)
+        for q in range(2):
+            build_edge(V2, PAD2, R2, W2, 0, True, q)
     with scope("dx2e"):
         dx_loop(V2, wt2, (early,), blocks2, M2, more2)
     with scope("dw2e"):
         dw(1, hT, V2, cells2, (early,))
     with scope("halo2l"):
-        build_edge(V2, PAD2, R2, W2, 0, False)
+        build_edge(V2, PAD2, R2, W2, 0, False, 0)
     with scope("dx2l"):
-        dx_loop(V2, wt2, (late,), blocks2, M2, mask2)
-    with scope("pack1"):
-        pack(V1, PAD1, S1, W1)
-    halo1 = send_halo(S1, R1, 2)
+        dx_loop(V2, wt2, (late,), ((0, 768, ((1, 96),)), (768, 768, ((2, 0),))), M2, more2)
+    with scope("halo2m"):
+        build_edge(V2, PAD2, R2, W2, 0, False, 1)
+    for q, b in enumerate(((0, 768, ((0, 960),)), (768, 768, ((1, 864),)))):
+        with scope("dx2m%d" % q):
+            dx_loop(V2, wt2, (late,), (b,), M2, mask2)
+        with scope("pack1%d" % q):
+            pack(V1, PAD1, S1, W1, halves[q])
+        send_halo(S1, R1, 1, q)
     with scope("dw2l"):
         dw(1, hT, V2, cells2, (late,))
 
@@ -244,6 +270,18 @@
             rows = pl.ds(pl.multiple_of((2 * j + 1 - core) * BLOCK, 16), BLOCK)
             remote(wb.at[g, rows], recvA.at[g, j], as_.at[g], ar.at[g], partner, dp)
         sent.append((recvA.at[g], as_.at[g]))
+
+    def send_taps(ready):
+        for v in range(2):
+            @pl.when(core == v)
+            def _(v=v):
+                for c in (1, 2 * v) if ready else (2 - 2 * v,):
+                    for k in (c, 3 + c, 6 + c):
+                        for b in range(1 - v, LONS, 2):
+                            lo, hi = max(k * CH, b * BLOCK), min((k + 1) * CH, (b + 1) * BLOCK)
+                            if lo < hi:
+                                remote(wb.at[0, lo:hi], recvA.at[0, b // 2, lo - b * BLOCK:hi - b * BLOCK],
+                                       as_.at[0], ar.at[0], partner, dp)
 
     def stage_b(g):
         wait_all(recvA.at[g], ar.at[g])
@@ -324,27 +362,32 @@
     stage_a(1)
     with scope("inner1"):
         build_inner(V1, PAD1, W1)
-    with scope("dx1c"):
-        dx_loop(V1, wt1, (1,), blocks1, M1, first1)
     with scope("dw1c"):
         dw(0, xT, V1, cells1, (1,))
     with scope("halo1e"):
-        build_edge(V1, PAD1, R1, W1, 2, True)
+        for q in range(2):
+            build_edge(V1, PAD1, R1, W1, 1, True, q)
     with scope("dw1e"):
         dw(0, xT, V1, cells1, (early,))
-    with scope("dx1e"):
-        dx_loop(V1, wt1, (early,), blocks1, M1, more1)
+    send_taps(True)
     with scope("halo1l"):
-        build_edge(V1, PAD1, R1, W1, 2, False)
+        build_edge(V1, PAD1, R1, W1, 1, False, 0)
     with scope("dw1l"):
-        dw(0, xT, V1, cells1, (late,))
-    stage_a(0)
+        dw_part(((0, 128, 640), (0, 768, 64), (512, 768, 0)), False)
+    with scope("halo1m"):
+        build_edge(V1, PAD1, R1, W1, 1, False, 1)
+    with scope("dw1m"):
+        dw_part(((128, 896, 768), (768, 768, 832), (1280, 256, 768)), True)
+    send_taps(False)
+    sent.append((recvA.at[0], as_.at[0]))
     with scope("b2"):
         stage_b(1)
-    with scope("dx1l"):
-        dx_loop(V1, wt1, (late,), blocks1, M1, last1)
+    with scope("dx1a"):
+        dx_loop(V1, wt1, (0, 1, 2), blocks1[:2], M1, only1)
     with scope("b1"):
         stage_b(0)
+    with scope("dx1b"):
+        dx_loop(V1, wt1, (0, 1, 2), blocks1[2:], M1, only1)
     with scope("c2y"):
         stage_cy(1)
     with scope("c2x"):
@@ -364,8 +407,6 @@
     with scope("f1"):
         finish(0, g1)
     with scope("sends"):
-        for c in halo2 + halo1:
-            c.wait_send()
         for ref, sem in sent:
             wait_all(ref, sem)
 
@@ -413,7 +454,7 @@
             V((2, 3, TOP, HALF), BF), V((2, 3, REST, HALF), BF),
             V((BLOCK + 16, HALF), F32),
             V((2, DPS, 16, HALF), BF), V((2, DPS - 1, 16, HALF), BF),
-            D((5,)), D((4,)), D((4,)), D((2,)), D((2,)), D((2, 2)), D((2, 2)),
+            D((5,)), D((2, 2)), D((2, 2, 2)), D((2,)), D((2,)), D((2, 2)), D((2, 2)),
             D((2, 2)), D((2, 2)), D((2,)), D((2,)),
             pltpu.SemaphoreType.REGULAR, pltpu.SemaphoreType.REGULAR,
         ],

time: 42.5 us -> 41.8 us (0.984)
  the two profiles are of different devices: /device:TPU:2 before, /device:TPU:8 now
where the time goes in v3:
time: 41.8 us; the launch traced here: 41.7 us
  Pallas kernels  41.1 us (98%)
  between operations  0.64 us (2%)
    pallas_call x1, Pallas kernels, local(): pl.pallas_call(kernel, name='conv_back', out_shape=outs, in_specs=[hbm] *...  40.2 us
    pallas_call x1, Pallas kernels, local(): pl.pallas_call(write_out, name='write_out', out_shape=outs, in_specs=[vm]...  0.92 us

profile of v3, /device:TPU:8, one launch (start us, length us, event | category | flops | bytes accessed | tf_op | source)
XLA Modules:
  0.0 41.7 jit_solution(8958819369536116219)
XLA Ops:
  0.6 40.2 %conv_back.1 = (bf16[1536,256]{1,0:T(8,128)(2,1)S(1)}, f32[2304]{0:T(1024)S(1)}, f32[2304]{0:T(1024)S(1)}) custom-call(bf16[1536,256]{1,0:T(8,128)(2,1)} %bitcast.4, bf16[1536,256]{1,0:T(8,128)(2,1)} %bitcast.5, bf16[1536,256]{1,0:T(8,128)(2,1)} %bitcast.6, bf16[2304,256]{1,0:T(8,128)(2,1)} %w1.1, bf16[2304,256]{1,0:T(8,128)(2,1)} %w2.1), custom_call_target="tpu_custom_call" | custom-call | tf_op jit(solution)/shard_map/conv_back/pallas_call | solution.py:434
  40.8 0.9 %write_out.1 = (bf16[1536,256]{1,0:T(8,128)(2,1)}, f32[2304]{0:T(1024)}, f32[2304]{0:T(1024)}) custom-call(bf16[1536,256]{1,0:T(8,128)(2,1)S(1)} %get-tuple-element.9.dx, f32[2304]{0:T(1024)S(1)} %get-tuple-element.10.g1, f32[2304]{0:T(1024)S(1)} %get-tuple-element.11.g2), custom_call_target="tpu_custom_call" | custom-call | tf_op jit(solution)/shard_map/write_out/pallas_call | solution.py:465

commit v4 on v3

--- a/solution.py
+++ b/solution.py
@@ -93,6 +93,9 @@
         pltpu.make_async_copy(ref, ref, sem).wait()
 
     sent = []
+    for g in range(2):
+        sent.extend(((rX1.at[g], xs.at[g, 0]), (rY1.at[g], ys.at[g, 0])))
+    at_wrap = (lon == 0) | (lon == 7) | (lon == 8) | (lon == 15)
 
     halves = (range(0, LAT // 2), range(LAT // 2, LAT))
 
@@ -300,8 +303,6 @@
             remote(sX.at[g, h, l], rX1.at[g, e], xs.at[g, 0], xr.at[g, 0], *xid[e])
         for d in (1, 0, 2):
             remote(sY.at[g, :, ypeer[d]], rY1.at[g, d], ys.at[g, 0], yr.at[g, 0], ylon[d], dp)
-        sent.extend(((rX1.at[g], xs.at[g, 0]), (rY1.at[g], ys.at[g, 0])))
-
     def stage_cy(g):
         wait_all(rY1.at[g], yr.at[g, 0])
         for h in range(2):
@@ -370,6 +371,10 @@
     with scope("dw1e"):
         dw(0, xT, V1, cells1, (early,))
     send_taps(True)
+    @pl.when(at_wrap)
+    def _():
+        stage_b(1)
+
     with scope("halo1l"):
         build_edge(V1, PAD1, R1, W1, 1, False, 0)
     with scope("dw1l"):
@@ -380,14 +385,16 @@
         dw_part(((128, 896, 768), (768, 768, 832), (1280, 256, 768)), True)
     send_taps(False)
     sent.append((recvA.at[0], as_.at[0]))
-    with scope("b2"):
+    @pl.when(jnp.logical_not(at_wrap))
+    def _():
         stage_b(1)
+
     with scope("dx1a"):
-        dx_loop(V1, wt1, (0, 1, 2), blocks1[:2], M1, only1)
+        dx_loop(V1, wt1, (0, 1, 2), blocks1[:1], M1, only1)
     with scope("b1"):
         stage_b(0)
     with scope("dx1b"):
-        dx_loop(V1, wt1, (0, 1, 2), blocks1[2:], M1, only1)
+        dx_loop(V1, wt1, (0, 1, 2), blocks1[1:], M1, only1)
     with scope("c2y"):
         stage_cy(1)
     with scope("c2x"):

time: 41.8 us -> 40.2 us (0.962)
  the two profiles are of different devices: /device:TPU:8 before, /device:TPU:2 now
where the time goes in v4:
time: 40.2 us; the launch traced here: 40 us
  Pallas kernels  39.4 us (98%)
  between operations  0.64 us (2%)
    pallas_call x1, Pallas kernels, local(): pl.pallas_call(kernel, name='conv_back', out_shape=outs, in_specs=[hbm] *...  38.5 us
    pallas_call x1, Pallas kernels, local(): pl.pallas_call(write_out, name='write_out', out_shape=outs, in_specs=[vm]...  0.92 us

profile of v4, /device:TPU:2, one launch (start us, length us, event | category | flops | bytes accessed | tf_op | source)
XLA Modules:
  0.0 40.0 jit_solution(9541714635489669009)
XLA Ops:
  0.6 38.5 %conv_back.1 = (bf16[1536,256]{1,0:T(8,128)(2,1)S(1)}, f32[2304]{0:T(1024)S(1)}, f32[2304]{0:T(1024)S(1)}) custom-call(bf16[1536,256]{1,0:T(8,128)(2,1)} %bitcast.4, bf16[1536,256]{1,0:T(8,128)(2,1)} %bitcast.5, bf16[1536,256]{1,0:T(8,128)(2,1)} %bitcast.6, bf16[2304,256]{1,0:T(8,128)(2,1)} %w1.1, bf16[2304,256]{1,0:T(8,128)(2,1)} %w2.1), custom_call_target="tpu_custom_call" | custom-call | tf_op jit(solution)/shard_map/conv_back/pallas_call | solution.py:441
  39.1 0.9 %write_out.1 = (bf16[1536,256]{1,0:T(8,128)(2,1)}, f32[2304]{0:T(1024)}, f32[2304]{0:T(1024)}) custom-call(bf16[1536,256]{1,0:T(8,128)(2,1)S(1)} %get-tuple-element.9.dx, f32[2304]{0:T(1024)S(1)} %get-tuple-element.10.g1, f32[2304]{0:T(1024)S(1)} %get-tuple-element.11.g2), custom_call_target="tpu_custom_call" | custom-call | tf_op jit(solution)/shard_map/write_out/pallas_call | solution.py:472

commit v5 on v4

--- a/solution.py
+++ b/solution.py
@@ -389,12 +389,10 @@
     def _():
         stage_b(1)
 
-    with scope("dx1a"):
-        dx_loop(V1, wt1, (0, 1, 2), blocks1[:1], M1, only1)
     with scope("b1"):
         stage_b(0)
     with scope("dx1b"):
-        dx_loop(V1, wt1, (0, 1, 2), blocks1[1:], M1, only1)
+        dx_loop(V1, wt1, (0, 1, 2), blocks1[:], M1, only1)
     with scope("c2y"):
         stage_cy(1)
     with scope("c2x"):

time: 40.2 us -> 39.9 us (level)
  no operation moved by 1% of the time
where the time goes in v5:
time: 39.9 us; the launch traced here: 39.8 us
  Pallas kernels  39.1 us (98%)
  between operations  0.64 us (2%)
    pallas_call x1, Pallas kernels, local(): pl.pallas_call(kernel, name='conv_back', out_shape=outs, in_specs=[hbm] *...  38.2 us
    pallas_call x1, Pallas kernels, local(): pl.pallas_call(write_out, name='write_out', out_shape=outs, in_specs=[vm]...  0.92 us

profile of v5, /device:TPU:2, one launch (start us, length us, event | category | flops | bytes accessed | tf_op | source)
XLA Modules:
  0.0 39.8 jit_solution(6403062582632239102)
XLA Ops:
  0.6 38.2 %conv_back.1 = (bf16[1536,256]{1,0:T(8,128)(2,1)S(1)}, f32[2304]{0:T(1024)S(1)}, f32[2304]{0:T(1024)S(1)}) custom-call(bf16[1536,256]{1,0:T(8,128)(2,1)} %bitcast.4, bf16[1536,256]{1,0:T(8,128)(2,1)} %bitcast.5, bf16[1536,256]{1,0:T(8,128)(2,1)} %bitcast.6, bf16[2304,256]{1,0:T(8,128)(2,1)} %w1.1, bf16[2304,256]{1,0:T(8,128)(2,1)} %w2.1), custom_call_target="tpu_custom_call" | custom-call | tf_op jit(solution)/shard_map/conv_back/pallas_call | solution.py:439
  38.9 0.9 %write_out.1 = (bf16[1536,256]{1,0:T(8,128)(2,1)}, f32[2304]{0:T(1024)}, f32[2304]{0:T(1024)}) custom-call(bf16[1536,256]{1,0:T(8,128)(2,1)S(1)} %get-tuple-element.9.dx, f32[2304]{0:T(1024)S(1)} %get-tuple-element.10.g1, f32[2304]{0:T(1024)S(1)} %get-tuple-element.11.g2), custom_call_target="tpu_custom_call" | custom-call | tf_op jit(solution)/shard_map/write_out/pallas_call | solution.py:470
